TPU v7x, 128 devices: a whole 4x4x4 slice. The times are simulated.
128 devices in a mesh: row: 8 (over z, core), col: 16 (over x, y).
Axes of the slice: x: 4, y: 4, z: 4, core: 2. Of those that a mesh axis runs over, the one named last changes fastest.
Arguments:
- tiles: bfloat16 [8, 16, 128, 128, 128], P('row', 'col'), may hold values from -6 to 6
- tile_row: int32 [8, 16, 128], P('row', 'col'), may hold values from 0 to 127, as said below
- tile_col: int32 [8, 16, 128], P('row', 'col'), may hold values from 0 to 63
- tile_count: int32 [8, 16], P('row', 'col'), may hold values from 16 to 128, as said below
- query_ids: int32 [128], replicated, may hold values from 0 to 131071
- damping: float32 [128], replicated, may hold values from 0.006629126 to 0.026516505
Outputs:
- scores: float32 [131072, 128], P(('row', 'col'))
Inputs may be any that keep to these rules, and one draw needn't show every extreme that they name: `tile_count`: some device holds exactly 128 live slots; slots at or past the count hold arbitrary finite values and are ignored. `tile_row`: positions may repeat within a device; such tiles add. For every device and every col index o, the live slots name at most 4 distinct values among o * 8 to o * 8 + 7, and every device reaches 4 for some o. `query_ids`: ids may repeat.
All inputs are finite; a program needn't handle non-finite values.
Results may differ from a plain program's by a relative error of at most 0.003.
Values may be sent and summed in bfloat16 or wider, within the bound.
A program may use at most 128 MiB of HBM per device.

v0:
```python
import math

import jax
import jax.numpy as jnp
from jax import lax
from jax.sharding import PartitionSpec as P

BPD = 8
TERMS = 4
TOUCH = 4


def sent_to_all(value, axis):
    copies = jnp.broadcast_to(value, (lax.axis_size(axis), *value.shape))
    return lax.all_to_all(copies, axis, split_axis=0, concat_axis=0, tiled=True)


def in_order(blocks, dim):
    blocks = jnp.moveaxis(blocks, 0, dim)
    dims = blocks.shape
    return blocks.reshape(*dims[:dim], dims[dim] * dims[dim + 1], *dims[dim + 2 :])


def gathered_copies(value, axis, dim):
    blocks = sent_to_all(value, axis)
    return in_order(blocks, dim)


def counted_partial(tile_block, rows, cols, count, xcol, row_blocks):
    slots, tile = (tile_block.shape[0], tile_block.shape[1])
    width = xcol.shape[2]
    group = math.gcd(slots, 64)
    groups_live = (count + group - 1) // group

    def add_group(index, total):
        start = index * group
        tgroup = lax.dynamic_slice_in_dim(tile_block, start, group, 0)
        rgroup = lax.dynamic_slice_in_dim(rows, start, group, 0)
        cgroup = lax.dynamic_slice_in_dim(cols, start, group, 0)
        prod = jnp.einsum("tab,tbq->taq", tgroup, xcol[cgroup], preferred_element_type=jnp.float32)
        live = (start + jnp.arange(group, dtype=jnp.int32) < count).astype(jnp.float32)
        return total.at[rgroup].add(prod * live[:, None, None])

    start_total = jnp.zeros((row_blocks, tile, width), jnp.float32)
    return lax.fori_loop(0, groups_live, add_group, start_total)


def touched_sum(part, rows, count, n_col):
    row_blocks, tile, width = part.shape
    live = jnp.arange(rows.shape[0], dtype=jnp.int32) < count
    hits = (rows[None, :] == jnp.arange(row_blocks, dtype=jnp.int32)[:, None]) & live[None, :]
    marked = jnp.any(hits, axis=1).reshape(n_col, BPD)
    rank = jnp.cumsum(marked.astype(jnp.int32), axis=1) - 1
    places = jnp.arange(TOUCH, dtype=jnp.int32)
    select = marked[:, None, :] & (rank[:, None, :] == places[None, :, None])
    rounded = part.astype(jnp.bfloat16).reshape(n_col, BPD, tile, width)
    blocks = jnp.einsum(
        "ojb,obtq->ojtq", select.astype(jnp.bfloat16), rounded, preferred_element_type=jnp.float32
    ).astype(jnp.bfloat16)
    local = jnp.arange(BPD, dtype=jnp.int32)
    block_ids = jnp.sum(select.astype(jnp.int32) * (local[None, None, :] + 1), axis=2) - 1
    got_blocks, got_ids = (
        lax.all_to_all(blocks, "col", split_axis=0, concat_axis=0, tiled=True),
        lax.all_to_all(block_ids, "col", split_axis=0, concat_axis=0, tiled=True),
    )
    placing = (got_ids[:, :, None] == local[None, None, :]).astype(jnp.bfloat16)
    return jnp.einsum("sjb,sjtq->btq", placing, got_blocks, preferred_element_type=jnp.float32)


def shards(tiles, tile_row, tile_col, tile_count, query_ids, damping):
    tile_block = tiles[0, 0]
    rows = tile_row[0, 0]
    cols = tile_col[0, 0]
    count = tile_count[0, 0]
    tile = tile_block.shape[1]
    queries = query_ids.shape[0]
    n_row = lax.axis_size("row")
    n_col = lax.axis_size("col")
    col_index = lax.axis_index("col")
    row_blocks = BPD * n_col
    col_blocks = BPD * n_row
    block_ids = jnp.arange(col_blocks, dtype=jnp.int32)
    global_block = (block_ids // BPD * n_col + col_index) * BPD + block_ids % BPD
    node_ids = global_block[:, None] * tile + jnp.arange(tile, dtype=jnp.int32)[None, :]
    xcol = (node_ids[:, :, None] == query_ids[None, None, :]).astype(jnp.bfloat16)
    scores = jnp.zeros((BPD, tile, queries), jnp.float32)
    coef = jnp.ones((queries,), jnp.float32)
    for step in range(TERMS):
        part = counted_partial(tile_block, rows, cols, count, xcol, row_blocks)
        owned = touched_sum(part, rows, count, n_col)
        scores = scores + coef[None, None, :] * owned
        coef = coef * damping
        if step + 1 < TERMS:
            xcol = gathered_copies(owned.astype(jnp.bfloat16), "row", 0)
    return scores.reshape(BPD * tile, queries)


def solution(mesh):
    in_specs = (
        P("row", "col", None, None, None),
        P("row", "col", None),
        P("row", "col", None),
        P("row", "col"),
        P(),
        P(),
    )
    out_specs = P(("row", "col"), None)
    return jax.shard_map(shards, mesh=mesh, in_specs=in_specs, out_specs=out_specs, check_vma=False)
```

profile of v0, /device:TPU:0, one launch (start us, length us, event | category | flops | bytes accessed | tf_op | source)
XLA Modules:
  0.0 479.8 jit_solution(5692092447900166917)
XLA Ops:
  2.9 7.1 %all-to-all-start = ((s32[16,1,4]{2,1,0:T(1,128)}), s32[16,1,4]{2,1,0:T(1,128)S(1)}, u32[]{:S(2)}, u32[]{:S(2)}) async-start(s32[16,1,4]{2,1,0:T(1,128)} %copy.59), calls=%async_computation | async-start | bytes 16384 | tf_op jit(solution)/shard_map/all_to_all | solution.py:64
  10.1 4.3 broadcast.198.clone.2
  14.4 23.8 %while.44 = (s32[]{:T(128)}, f32[128,128,128]{2,1,0:T(8,128)}, s32[]{:T(128)}, s32[128]{0:T(128)S(1)}, bf16[128,128,128]{2,1,0:T(8,128)(2,1)}, /*index=5*/s32[12...) while((s32[]{:T(128)}, f32[128,128,128]{2,1,0:T(8,128)}, ...), condition=%wide.region_5.6_spmd.clone, body=%wide.region_3.5_spmd.clone.sunk | while | flops 272631360 | bytes 27302844 | solution.py:45
  14.5 2.7 compare_convert_fusion.13
  17.2 2.5 gather_fusion.3
  20.4 4.3 convolution_multiply_fusion.11
  24.7 13.6 %scatter_fusion.3 = f32[128,128,128]{2,1,0:T(8,128)} fusion(f32[128,128,128]{2,1,0:T(8,128)} %get-tuple-element.522, s32[64]{0:T(128)S(1)} %get-tuple-element.506, f32[64,128,128]{2,1,0:T(8,128)} %convolution_multiply_fusion.11), kind=kCustom, calls=%fused_computation.4.clone.clone.1 | custom fusion | flops 1048576 | bytes 12583168 | tf_op jit(solution)/shard_map/while/body/scatter-add | solution.py:42
  38.3 4.4 convert_element_type.88
  42.6 4.1 fusion.26
  46.7 29.1 %all-to-all-start.1 = ((bf16[16,4,128,128]{3,1,2,0:T(4,128)(2,1)}), bf16[16,4,128,128]{3,1,2,0:T(4,128)(2,1)S(1)}, u32[]{:S(2)}, u32[]{:S(2)}) async-start(bf16[16,4,128,128]{3,1,2,0:T(4,128)(2,1)} %fusion.26), calls=%async_computation.1 | async-start | bytes 4194304 | tf_op jit(solution)/shard_map/all_to_all | solution.py:63
  76.0 30.7 %all-to-all-done.1 = bf16[16,4,128,128]{3,1,2,0:T(4,128)(2,1)S(1)} async-done(((bf16[16,4,128,128]{3,1,2,0:T(4,128)(2,1)}), bf16[16,4,128,128]{3,1,2,0:T(4,128)(2,1)S(1)}, u32[]{:S(2)}, u32[]{:S(2)}) %all-to-all-start.1) | async-done | bytes 2097184 | tf_op jit(solution)/shard_map/all_to_all | solution.py:63
  107.9 1.8 broadcast_in_dim.28
  109.8 5.9 %all-to-all-start.2 = ((bf16[8,8,128,128]{3,2,1,0:T(8,128)(2,1)}), bf16[8,8,128,128]{3,2,1,0:T(8,128)(2,1)S(1)}, u32[]{:S(2)}, u32[]{:S(2)}) async-start(bf16[8,8,128,128]{3,2,1,0:T(8,128)(2,1)} %broadcast_in_dim.28), calls=%async_computation.2 | async-start | bytes 4194304 | tf_op jit(solution)/shard_map/all_to_all | solution.py:15
  115.6 27.2 %all-to-all-done.2 = bf16[8,8,128,128]{3,2,1,0:T(8,128)(2,1)S(1)} async-done(((bf16[8,8,128,128]{3,2,1,0:T(8,128)(2,1)}), bf16[8,8,128,128]{3,2,1,0:T(8,128)(2,1)S(1)}, u32[]{:S(2)}, u32[]{:S(2)}) %all-to-all-start.2) | async-done | bytes 2097184 | tf_op jit(solution)/shard_map/all_to_all | solution.py:15
  142.8 4.3 broadcast.198.clone.1
  147.1 22.5 %while.41 = (s32[]{:T(128)}, f32[128,128,128]{2,1,0:T(8,128)}, s32[]{:T(128)}, s32[128]{0:T(128)S(1)}, bf16[128,128,128]{2,1,0:T(8,128)(2,1)}, /*index=5*/s32[12...) while((s32[]{:T(128)}, f32[128,128,128]{2,1,0:T(8,128)}, ...), condition=%wide.region_8.9_spmd, body=%wide.region_6.8_spmd.sunk | while | flops 270534208 | bytes 41949676 | solution.py:45
  147.2 1.2 copy-done.2
  148.4 2.5 gather_fusion
  151.6 4.3 convolution_multiply_fusion.8
  155.9 13.6 %scatter_fusion = f32[128,128,128]{2,1,0:T(8,128)} fusion(f32[128,128,128]{2,1,0:T(8,128)} %get-tuple-element.560, s32[64]{0:T(128)S(1)} %get-tuple-element.475, f32[64,128,128]{2,1,0:T(8,128)} %convolution_multiply_fusion.8), kind=kCustom, calls=%fused_computation.5.clone.1 | custom fusion | flops 1048576 | bytes 12583168 | tf_op jit(solution)/shard_map/while/body/scatter-add | solution.py:42
  169.5 4.4 convert_element_type.91
  173.9 2.8 fusion.29
  176.7 53.6 %all_to_all.44 = bf16[16,4,128,128]{3,1,2,0:T(4,128)(2,1)S(1)} all-to-all(bf16[16,4,128,128]{3,1,2,0:T(4,128)(2,1)S(1)} %fusion.29), channel_id=1, replica_groups=mesh['row'=8,'col'=16] {'col'}, dimensions={0} | all-to-all | bytes 4194304 | tf_op jit(solution)/shard_map/all_to_all | solution.py:63
  231.5 1.8 broadcast_in_dim.29
  233.4 3.6 all-to-all-start.4
  237.0 27.1 %all-to-all-done.4 = bf16[8,8,128,128]{3,2,1,0:T(8,128)(2,1)S(1)} async-done(((bf16[8,8,128,128]{3,2,1,0:T(8,128)(2,1)}), bf16[8,8,128,128]{3,2,1,0:T(8,128)(2,1)S(1)}, u32[]{:S(2)}, u32[]{:S(2)}) %all-to-all-start.4) | async-done | bytes 2097184 | tf_op jit(solution)/shard_map/all_to_all | solution.py:15
  264.1 4.3 broadcast.198.clone
  268.4 22.5 %while.42 = (s32[]{:T(128)}, f32[128,128,128]{2,1,0:T(8,128)}, s32[]{:T(128)}, s32[128]{0:T(128)S(1)}, bf16[128,128,128]{2,1,0:T(8,128)(2,1)}, /*index=5*/s32[12...) while((s32[]{:T(128)}, f32[128,128,128]{2,1,0:T(8,128)}, ...), condition=%wide.region_11.12_spmd, body=%wide.region_9.11_spmd.sunk | while | flops 270534208 | bytes 41949676 | solution.py:45
  269.7 2.5 gather_fusion.1
  272.9 4.3 convolution_multiply_fusion.9
  277.2 13.6 %scatter_fusion.1 = f32[128,128,128]{2,1,0:T(8,128)} fusion(f32[128,128,128]{2,1,0:T(8,128)} %get-tuple-element.596, s32[64]{0:T(128)S(1)} %get-tuple-element.485, f32[64,128,128]{2,1,0:T(8,128)} %convolution_multiply_fusion.9), kind=kCustom, calls=%fused_computation.6.clone.1 | custom fusion | flops 1048576 | bytes 12583168 | tf_op jit(solution)/shard_map/while/body/scatter-add | solution.py:42
  290.8 4.4 convert_element_type.94
  295.2 2.8 fusion.32
  298.0 53.2 %all_to_all.45 = bf16[16,4,128,128]{3,1,2,0:T(4,128)(2,1)S(1)} all-to-all(bf16[16,4,128,128]{3,1,2,0:T(4,128)(2,1)S(1)} %fusion.32), channel_id=1, replica_groups=mesh['row'=8,'col'=16] {'col'}, dimensions={0} | all-to-all | bytes 4194304 | tf_op jit(solution)/shard_map/all_to_all | solution.py:63
  351.2 2.0 fusion.83
  353.3 1.8 broadcast_in_dim.30
  355.1 3.6 all-to-all-start.6
  358.7 27.1 %all-to-all-done.6 = bf16[8,8,128,128]{3,2,1,0:T(8,128)(2,1)S(1)} async-done(((bf16[8,8,128,128]{3,2,1,0:T(8,128)(2,1)}), bf16[8,8,128,128]{3,2,1,0:T(8,128)(2,1)S(1)}, u32[]{:S(2)}, u32[]{:S(2)}) %all-to-all-start.6) | async-done | bytes 2097184 | tf_op jit(solution)/shard_map/all_to_all | solution.py:15
  385.8 4.3 broadcast.198
  390.1 22.5 %while.43 = (s32[]{:T(128)}, f32[128,128,128]{2,1,0:T(8,128)}, s32[]{:T(128)}, s32[128]{0:T(128)S(1)}, bf16[128,128,128]{2,1,0:T(8,128)(2,1)}, /*index=5*/s32[12...) while((s32[]{:T(128)}, f32[128,128,128]{2,1,0:T(8,128)}, ...), condition=%wide.region_14.15_spmd, body=%wide.region_12.14_spmd.sunk | while | flops 270534208 | bytes 41949676 | solution.py:45
  391.4 2.5 gather_fusion.2
  394.6 4.3 convolution_multiply_fusion.10
  398.9 13.6 %scatter_fusion.2 = f32[128,128,128]{2,1,0:T(8,128)} fusion(f32[128,128,128]{2,1,0:T(8,128)} %get-tuple-element.632, s32[64]{0:T(128)S(1)} %get-tuple-element.495, f32[64,128,128]{2,1,0:T(8,128)} %convolution_multiply_fusion.10), kind=kCustom, calls=%fused_computation.7.clone.1 | custom fusion | flops 1048576 | bytes 12583168 | tf_op jit(solution)/shard_map/while/body/scatter-add | solution.py:42
  412.6 4.4 convert_element_type.97
  416.9 4.1 fusion.35
  421.0 24.9 %all-to-all-start.7 = ((bf16[16,4,128,128]{3,1,2,0:T(4,128)(2,1)}), bf16[16,4,128,128]{3,1,2,0:T(4,128)(2,1)S(1)}, u32[]{:S(2)}, u32[]{:S(2)}) async-start(bf16[16,4,128,128]{3,1,2,0:T(4,128)(2,1)} %fusion.35), calls=%async_computation.7 | async-start | bytes 4194304 | tf_op jit(solution)/shard_map/all_to_all | solution.py:63
  445.9 30.7 %all-to-all-done.7 = bf16[16,4,128,128]{3,1,2,0:T(4,128)(2,1)S(1)} async-done(((bf16[16,4,128,128]{3,1,2,0:T(4,128)(2,1)}), bf16[16,4,128,128]{3,1,2,0:T(4,128)(2,1)S(1)}, u32[]{:S(2)}, u32[]{:S(2)}) %all-to-all-start.7) | async-done | bytes 2097184 | tf_op jit(solution)/shard_map/all_to_all | solution.py:63
  476.6 2.3 fusion.53
  (53 shorter events, 11.3 us)
Async XLA Ops:
  2.9 43.9 %all-to-all-start = ((s32[16,1,4]{2,1,0:T(1,128)}), s32[16,1,4]{2,1,0:T(1,128)S(1)}, u32[]{:S(2)}, u32[]{:S(2)}) async-start(s32[16,1,4]{2,1,0:T(1,128)} %copy.59), calls=%async_computation | async-start | bytes 16384 | tf_op jit(solution)/shard_map/all_to_all | solution.py:64
  10.1 4.3 copy-start.6
  10.1 4.3 copy-start.7
  10.1 4.3 copy-start.8
  46.7 59.9 %all-to-all-start.1 = ((bf16[16,4,128,128]{3,1,2,0:T(4,128)(2,1)}), bf16[16,4,128,128]{3,1,2,0:T(4,128)(2,1)S(1)}, u32[]{:S(2)}, u32[]{:S(2)}) async-start(bf16[16,4,128,128]{3,1,2,0:T(4,128)(2,1)} %fusion.26), calls=%async_computation.1 | async-start | bytes 4194304 | tf_op jit(solution)/shard_map/all_to_all | solution.py:63
  109.8 33.0 %all-to-all-start.2 = ((bf16[8,8,128,128]{3,2,1,0:T(8,128)(2,1)}), bf16[8,8,128,128]{3,2,1,0:T(8,128)(2,1)S(1)}, u32[]{:S(2)}, u32[]{:S(2)}) async-start(bf16[8,8,128,128]{3,2,1,0:T(8,128)(2,1)} %broadcast_in_dim.28), calls=%async_computation.2 | async-start | bytes 4194304 | tf_op jit(solution)/shard_map/all_to_all | solution.py:15
  147.1 1.3 copy-start.2
  155.9 13.7 %copy-start.3 = (bf16[64,128,128]{2,1,0:T(8,128)(2,1)S(1)}, bf16[64,128,128]{2,1,0:T(8,128)(2,1)}, u32[]{:S(2)}) copy-start(bf16[64,128,128]{2,1,0:T(8,128)(2,1)} %copy-done.2) | copy-start | bytes 6291460 | tf_op jit(solution)/shard_map/while
  233.4 30.7 %all-to-all-start.4 = ((bf16[8,8,128,128]{3,2,1,0:T(8,128)(2,1)}), bf16[8,8,128,128]{3,2,1,0:T(8,128)(2,1)S(1)}, u32[]{:S(2)}, u32[]{:S(2)}) async-start(bf16[8,8,128,128]{3,2,1,0:T(8,128)(2,1)} %broadcast_in_dim.29), calls=%async_computation.4 | async-start | bytes 4194304 | tf_op jit(solution)/shard_map/all_to_all | solution.py:15
  268.4 1.3 copy-start.4
  277.2 13.7 %copy-start.5 = (bf16[64,128,128]{2,1,0:T(8,128)(2,1)S(1)}, bf16[64,128,128]{2,1,0:T(8,128)(2,1)}, u32[]{:S(2)}) copy-start(bf16[64,128,128]{2,1,0:T(8,128)(2,1)} %copy-done.4) | copy-start | bytes 6291460 | tf_op jit(solution)/shard_map/while
  355.1 30.7 %all-to-all-start.6 = ((bf16[8,8,128,128]{3,2,1,0:T(8,128)(2,1)}), bf16[8,8,128,128]{3,2,1,0:T(8,128)(2,1)S(1)}, u32[]{:S(2)}, u32[]{:S(2)}) async-start(bf16[8,8,128,128]{3,2,1,0:T(8,128)(2,1)} %broadcast_in_dim.30), calls=%async_computation.6 | async-start | bytes 4194304 | tf_op jit(solution)/shard_map/all_to_all | solution.py:15
  390.1 1.3 copy-start
  398.9 13.7 %copy-start.1 = (bf16[64,128,128]{2,1,0:T(8,128)(2,1)S(1)}, bf16[64,128,128]{2,1,0:T(8,128)(2,1)}, u32[]{:S(2)}) copy-start(bf16[64,128,128]{2,1,0:T(8,128)(2,1)} %copy-done) | copy-start | bytes 6291460 | tf_op jit(solution)/shard_map/while
  416.9 29.0 %copy-start.9 = (f32[128]{0:T(128)S(1)}, f32[128]{0:T(128)}, u32[]{:S(2)}) copy-start(f32[128]{0:T(128)} %param.19) | copy-start | bytes 1540
  421.0 55.5 %all-to-all-start.7 = ((bf16[16,4,128,128]{3,1,2,0:T(4,128)(2,1)}), bf16[16,4,128,128]{3,1,2,0:T(4,128)(2,1)S(1)}, u32[]{:S(2)}, u32[]{:S(2)}) async-start(bf16[16,4,128,128]{3,1,2,0:T(4,128)(2,1)} %fusion.35), calls=%async_computation.7 | async-start | bytes 4194304 | tf_op jit(solution)/shard_map/all_to_all | solution.py:63
where the time goes:
time: 480 us
  waiting for transfers between devices  143 us (30%)
  blocking collectives  107 us (22%)
  other arithmetic  79 us (16%)
  starting transfers between devices  74.2 us (15%)
  local copies, waits for them, and re-layouts  38.5 us (8%)
  matrix products  37.7 us (8%)
    all_to_all x2, blocking collectives, touched_sum(): lax.all_to_all(blocks, 'col', split_axis=0, concat_axis=0, tiled=True)  107 us
    all_to_all x3, waiting for transfers between devices, sent_to_all(): return lax.all_to_all(copies, axis, split_axis=0, concat_axis=0, tiled=True)  81.4 us
    all_to_all x2, waiting for transfers between devices, touched_sum(): lax.all_to_all(blocks, 'col', split_axis=0, concat_axis=0, tiled=True)  61.3 us
    scatter-add x4, other arithmetic, add_group(): return total.at[rgroup].add(prod * live[:, None, None])  54.5 us
    all_to_all x2, starting transfers between devices, touched_sum(): lax.all_to_all(blocks, 'col', split_axis=0, concat_axis=0, tiled=True)  54 us
    convert_element_type x4, other arithmetic, touched_sum(): rounded = part.astype(jnp.bfloat16).reshape(n_col, BPD, tile, width)  17.4 us
    another operation x4, local copies, waits for them, and re-layouts  17.1 us
    dot_general x4, matrix products, add_group(): jnp.einsum('tab,tbq->taq', tgroup, xcol[cgroup], preferred_element_type=j...  17.1 us
  transfers between devices with their start and end apart: 6, of which 5 were waited for; matrix products, arithmetic and copies ran while one was open for 8% of the time, Pallas kernels for 0%

commit v1 on v0

v1 whole, which is shorter than its diff:
```python
import functools

import jax
import jax.numpy as jnp
from jax import lax
from jax.experimental import pallas as pl
from jax.experimental.pallas import tpu as pltpu
from jax.sharding import PartitionSpec as P

TERMS = 4
CHUNKS = 4
ROWS = 128 // CHUNKS
HALF = ROWS // 2
SLOTS = 128
NONE = 128
EMPTY = 48
UNROLL = 16
PERM, SCOL, KEEP, DEND, PKEND, SBASE, JIDX = range(7)
MESH = pl.DeviceIdType.MESH
BF16, F32, I32 = jnp.bfloat16, jnp.float32, jnp.int32


def down(row):
    return jnp.transpose(jnp.broadcast_to(row, (128, 128)))


def slot_tables(rows, cols, count, col_index):
    lane = lax.broadcasted_iota(I32, (128, 128), 1)
    sub = lax.broadcasted_iota(I32, (128, 128), 0)
    lane1 = lax.broadcasted_iota(I32, (1, 128), 1)
    key = jnp.where(lane1 < count, rows, 128)
    key_row = jnp.broadcast_to(key, (128, 128))
    key_col = down(key)

    def total(mask, value=1):
        return jnp.sum(jnp.where(mask, value, 0), axis=0, keepdims=True)

    earlier = (key_col == key_row) & (sub < lane)
    rank = total((key_col < key_row) | earlier)
    repeat = jnp.minimum(total(earlier), 1)
    place = down(rank) == lane
    perm = total(place, sub)
    scol = total(place, down(cols))
    keep = total(place, down(repeat))
    touched = total(key_col == lane) > 0
    upto = total(key_col <= lane)
    dend = jnp.where(touched, upto - 1, NONE)
    touched_col = down(touched.astype(I32)) > 0
    before = total(touched_col & ((sub >> 3) == (lane >> 3)) & (sub < lane))
    jidx = jnp.where(touched, before, 4)
    packed = touched_col & ((sub >> 3) == (lane >> 2)) & (down(before) == (lane & 3))
    ends = total(packed, down(upto))
    pkend = jnp.where(ends > 0, ends - 1, NONE)
    sbase = (((scol >> 3) * 16 + col_index) * 8 + (scol & 7)) * 128
    return jnp.concatenate([perm, scol, keep, dend, pkend, sbase, jidx, jidx], axis=0)


def kernel(tiles_hbm, trow, tcol, count, qids, damping, out, *scratch):
    scratch = list(scratch)
    take = lambda n: [scratch.pop(0) for _ in range(n)]
    raw, flip, tabv, tabs, metav, idxv, idxs, qmat, coef, own, score = take(11)
    run = take(CHUNKS)
    xg = [take(CHUNKS) for _ in range(2)]
    recv1 = [[take(2) for _ in range(CHUNKS)] for _ in range(2)]
    send1, send2, recv2 = take(3)
    tile_sem, copy_sem, meta_ss, meta_rs, ss1, rs1, ss2, rs2, zss, zrs, css, crs = take(12)

    row, col = lax.axis_index("row"), lax.axis_index("col")
    z, core = row // 2, row % 2
    x, y = col // 4, col % 4
    wrap = lambda v, d: (v + d) % 4
    along = (
        lambda d: {"row": row, "col": wrap(x, d) * 4 + y},
        lambda d: {"row": row, "col": x * 4 + wrap(y, d)},
    )
    up = lambda d: {"row": wrap(z, d) * 2 + core, "col": col}
    other = {"row": z * 2 + 1 - core, "col": col}

    load = pltpu.make_async_copy(tiles_hbm, raw, tile_sem)
    load.start()
    barrier = pltpu.get_barrier_semaphore()
    peers = [f(d) for f in (*along, up) for d in (1, 2, 3)] + [other]
    for peer in peers:
        pl.semaphore_signal(barrier, inc=1, device_id=peer, device_id_type=MESH)

    def remote(src, dst, send_sem, recv_sem, peer):
        return pltpu.make_async_remote_copy(
            src_ref=src, dst_ref=dst, send_sem=send_sem, recv_sem=recv_sem, device_id=peer, device_id_type=MESH
        )

    tabv[...] = slot_tables(trow[...], tcol[...], count[0, 0], col)
    to_scalar = pltpu.make_async_copy(tabv, tabs, copy_sem.at[0])
    to_scalar.start()
    lane = lax.broadcasted_iota(I32, (128, 128), 1)
    qmat[...] = down(qids[...]) - lane
    coef[...] = down(damping[...])
    for h in range(CHUNKS):
        run[h][NONE] = jnp.zeros((ROWS, 128), BF16)
        for parity in range(2):
            for half in range(2):
                recv1[parity][h][half][EMPTY] = jnp.zeros((HALF, 128), BF16)
    pl.semaphore_wait(barrier, len(peers))
    meta = []
    for half in range(2):
        for d in (1, 2, 3):
            at = half * 3 + d - 1
            meta.append(remote(tabv, metav.at[at], meta_ss.at[at], meta_rs.at[at], along[half](d)))
            meta[-1].start()
    to_scalar.wait()
    load.wait()

    def first_products():
        def body(step, total):
            for u in range(UNROLL // 2):
                s = step * (UNROLL // 2) + u
                tile = raw[tabs[PERM, s]]
                hot = (qmat[...] == tabs[SBASE, s]).astype(BF16)
                prod = lax.dot_general(hot, tile, (((1,), (1,)), ((), ())), preferred_element_type=F32)
                total = jnp.where(tabs[KEEP, s] > 0, prod + total, prod)
                rounded = total.astype(BF16)
                for h in range(CHUNKS):
                    run[h][s] = rounded[h * ROWS : (h + 1) * ROWS]
                flip[s] = jnp.transpose(tile)
            return total

        lax.fori_loop(0, SLOTS // (UNROLL // 2), body, jnp.zeros((128, 128), F32))

    def products(t, h):
        source = xg[(t - 1) % 2][h]

        def body(step, total):
            for u in range(UNROLL):
                s = step * UNROLL + u
                prod = jnp.dot(source[tabs[SCOL, s]], flip[s], preferred_element_type=F32)
                total = jnp.where(tabs[KEEP, s] > 0, prod + total, prod)
                run[h][s] = total.astype(BF16)
            return total

        lax.fori_loop(0, SLOTS // UNROLL, body, jnp.zeros((ROWS, 128), F32))

    copies = {}

    def step1(t, h, half, d):
        return remote(
            send1.at[h, half, d - 1],
            recv1[t % 2][h][half].at[pl.ds((d - 1) * 16, 16)],
            ss1.at[t % 2, h, half, d - 1],
            rs1.at[t % 2, h, half, d - 1],
            along[half](d),
        )

    def step2(t, h, half, e):
        return remote(
            send2.at[h, half, e - 1],
            recv2.at[t % 2, h, half, e - 1],
            ss2.at[t % 2, h, half, e - 1],
            rs2.at[t % 2, h, half, e - 1],
            along[1 - half](e),
        )

    def ship(t, h):
        def body(d, _):
            for half in range(2):
                rows = pl.ds(half * HALF, HALF)
                for e in range(4):
                    if half == 0:
                        dest = wrap(x, d) * 4 + wrap(y, e)
                    else:
                        dest = wrap(x, e) * 4 + wrap(y, d)
                    for j in range(4):
                        send1[h, half, d - 1, e * 4 + j] = run[h][tabs[PKEND, dest * 4 + j], rows, :]
                step1(t, h, half, d).start()
            return 0

        lax.fori_loop(1, 4, body, 0)

    def merge(t, h):
        for half in range(2):
            for d in (1, 2, 3):
                step1(t, h, half, d).wait()
            rows = pl.ds(half * HALF, HALF)
            got = recv1[t % 2][h][half]

            def summed(e, b):
                dest = x * 4 + wrap(y, e) if half == 0 else wrap(x, e) * 4 + y
                block = dest * 8 + b
                total = run[h][tabs[DEND, block], rows, :].astype(F32)
                for d in (1, 2, 3):
                    total = total + got[idxs[half * 3 + d - 1, block]].astype(F32)
                return total

            def body(e, _):
                for b in range(8):
                    send2[h, half, e - 1, b] = summed(e, b).astype(BF16)
                step2(t, h, half, e).start()
                return 0

            lax.fori_loop(1, 4, body, 0)

            def body_own(b, _):
                own[h, half, b] = summed(0, b)
                return 0

            lax.fori_loop(0, 8, body_own, 0)

    def finish(t, h):
        for half in range(2):
            for e in (1, 2, 3):
                step2(t, h, half, e).wait()
        base = pl.multiple_of(row * 8, 8)
        factors = []
        for half in range(2):
            queries = pl.ds(h * ROWS + half * HALF, HALF)
            factor = coef[queries, :]
            for _ in range(t - 1):
                factor = factor * coef[queries, :]
            factors.append(factor)

        def body(b, _):
            for half in range(2):
                queries = pl.ds(h * ROWS + half * HALF, HALF)
                total = own[h, half, b]
                for e in range(3):
                    total = total + recv2[t % 2, h, half, e, b].astype(F32)
                if t == 0:
                    score[b, queries, :] = total
                else:
                    score[b, queries, :] = score[b, queries, :] + factors[half] * total
                if t + 1 < TERMS:
                    xg[t % 2][h][base + b, pl.ds(half * HALF, HALF), :] = total.astype(BF16)
            return 0

        lax.fori_loop(0, 8, body, 0)
        if t + 1 < TERMS:
            mine = xg[t % 2][h].at[pl.ds(base, 8)]
            for d in (1, 2, 3):
                c = remote(mine, mine, zss.at[t % 2, h, d - 1], zrs.at[t % 2, h, d - 1], up(d))
                c.start()
                copies[3, t, h, d] = c
            c = remote(mine, mine, css.at[t % 2, h, 0], crs.at[t % 2, h, 0], other)
            c.start()
            copies[4, t, h, 0] = c

    def hand_on(t, h):
        for d in (1, 3, 2):
            copies[3, t, h, d].wait()
            source = pl.multiple_of((wrap(z, 4 - d) * 2 + core) * 8, 8)
            part = xg[t % 2][h].at[pl.ds(source, 8)]
            c = remote(part, part, css.at[t % 2, h, d], crs.at[t % 2, h, d], other)
            c.start()
            copies[4, t, h, d] = c

    def gathered(t, h):
        for d in range(4):
            copies[4, t, h, d].wait()

    first_products()
    for h in range(CHUNKS):
        ship(0, h)
    for c in meta:
        c.wait()
    lane1 = lax.broadcasted_iota(I32, (1, 128), 1)
    for half in range(2):
        for d in (1, 2, 3):
            place = metav[half * 3 + d - 1, JIDX : JIDX + 1, :]
            away = (((lane1 >> 3) & 3) - y + 4) & 3 if half == 0 else ((lane1 >> 5) - x + 4) & 3
            idxv[half * 3 + d - 1 : half * 3 + d, :] = jnp.where(place < 4, (d - 1) * 16 + away * 4 + place, EMPTY)
    idxv[6:8, :] = jnp.zeros((2, 128), I32)
    to_scalar = pltpu.make_async_copy(idxv, idxs, copy_sem.at[1])
    to_scalar.start()
    to_scalar.wait()
    for t in range(TERMS):
        for h in range(CHUNKS):
            merge(t, h)
        for h in range(CHUNKS):
            finish(t, h)
        if t + 1 < TERMS:
            for h in range(CHUNKS):
                hand_on(t, h)
            for h in range(CHUNKS):
                gathered(t, h)
                products(t + 1, h)
                ship(t + 1, h)
    for b in range(8):
        out[b * 128 : (b + 1) * 128, :] = jnp.transpose(score[b])


def shards(tiles, tile_row, tile_col, tile_count, query_ids, damping):
    vmem = pl.BlockSpec(memory_space=pltpu.VMEM)
    dma = pltpu.SemaphoreType.DMA
    return pl.pallas_call(
        kernel,
        out_shape=jax.ShapeDtypeStruct((1024, 128), F32),
        in_specs=[pl.BlockSpec(memory_space=pl.ANY), vmem, vmem, pl.BlockSpec(memory_space=pltpu.SMEM), vmem, vmem],
        out_specs=vmem,
        scratch_shapes=[
            pltpu.VMEM((SLOTS, 128, 128), BF16),
            pltpu.VMEM((SLOTS, 128, 128), BF16),
            pltpu.VMEM((8, 128), I32),
            pltpu.SMEM((8, 128), I32),
            pltpu.VMEM((6, 8, 128), I32),
            pltpu.VMEM((8, 128), I32),
            pltpu.SMEM((8, 128), I32),
            pltpu.VMEM((128, 128), I32),
            pltpu.VMEM((128, 128), F32),
            pltpu.VMEM((CHUNKS, 2, 8, HALF, 128), F32),
            pltpu.VMEM((8, 128, 128), F32),
            *[pltpu.VMEM((SLOTS + 1, ROWS, 128), BF16) for _ in range(CHUNKS)],
            *[pltpu.VMEM((64, ROWS, 128), BF16) for _ in range(2 * CHUNKS)],
            *[pltpu.VMEM((EMPTY + 1, HALF, 128), BF16) for _ in range(4 * CHUNKS)],
            pltpu.VMEM((CHUNKS, 2, 3, 16, HALF, 128), BF16),
            pltpu.VMEM((CHUNKS, 2, 3, 8, HALF, 128), BF16),
            pltpu.VMEM((2, CHUNKS, 2, 3, 8, HALF, 128), BF16),
            dma,
            dma((2,)),
            dma((6,)),
            dma((6,)),
            dma((2, CHUNKS, 2, 3)),
            dma((2, CHUNKS, 2, 3)),
            dma((2, CHUNKS, 2, 3)),
            dma((2, CHUNKS, 2, 3)),
            dma((2, CHUNKS, 3)),
            dma((2, CHUNKS, 3)),
            dma((2, CHUNKS, 4)),
            dma((2, CHUNKS, 4)),
        ],
        compiler_params=pltpu.CompilerParams(collective_id=0, has_side_effects=True, vmem_limit_bytes=60 * 2**20),
        name="katz",
    )(
        tiles.reshape(SLOTS, 128, 128),
        tile_row.reshape(1, SLOTS),
        tile_col.reshape(1, SLOTS),
        tile_count,
        query_ids.reshape(1, 128),
        damping.reshape(1, 128),
    )


def solution(mesh):
    in_specs = (
        P("row", "col", None, None, None),
        P("row", "col", None),
        P("row", "col", None),
        P("row", "col"),
        P(),
        P(),
    )
    out_specs = P(("row", "col"), None)
    return jax.shard_map(shards, mesh=mesh, in_specs=in_specs, out_specs=out_specs, check_vma=False)
```

time: 480 us -> 124 us (0.26)
  waiting for transfers between devices: 143 us -> 0 us
  Pallas kernels: 0 us -> 121 us
  blocking collectives: 107 us -> 0 us
  other arithmetic: 79 us -> 0 us
  starting transfers between devices: 74.2 us -> 0 us
  matrix products: 37.7 us -> 0 us
  local copies, waits for them, and re-layouts: 38.5 us -> 1.87 us
    all_to_all x6 -> x0, waiting for transfers between devices: 143 us -> none  [the longest x3 81.4 us: sent_to_all(): return lax.all_to_all(copies, axis, split_axis=0, concat_axis=0, tiled=True)]
    pallas_call x0 -> x1, Pallas kernels: none -> 121 us  [shards(): pl.pallas_call(kernel, out_shape=jax.ShapeDtypeStruct((1024, 128), F32),...]
    all_to_all x2 -> x0, blocking collectives: 107 us -> none  [touched_sum(): lax.all_to_all(blocks, 'col', split_axis=0, concat_axis=0, tiled=True)]
    all_to_all x6 -> x0, starting transfers between devices: 74.2 us -> none  [the longest x2 54 us: touched_sum(): lax.all_to_all(blocks, 'col', split_axis=0, concat_axis=0, tiled=True)]
    scatter-add x4 -> x0, other arithmetic: 54.5 us -> none  [add_group(): return total.at[rgroup].add(prod * live[:, None, None])]
    dot_general x12 -> x0, matrix products: 37.7 us -> none  [the longest x4 17.1 us: add_group(): jnp.einsum('tab,tbq->taq', tgroup, xcol[cgroup], preferred_element_type=j...]
    convert_element_type x10 -> x0, other arithmetic: 22.7 us -> none  [the longest x4 17.4 us: touched_sum(): rounded = part.astype(jnp.bfloat16).reshape(n_col, BPD, tile, width)]
    another operation x4 -> x0, local copies, waits for them, and re-layouts: 17.1 us -> none
  transfers between devices with their start and end apart: 6 -> 0, of which waited for: 5 -> 0; matrix products, arithmetic and copies ran while one was open for 8% -> 0% of each run, Pallas kernels for 0% -> 0%
where the time goes in v1:
time: 124 us
  Pallas kernels  121 us (98%)
  local copies, waits for them, and re-layouts  1.87 us (2%)
    pallas_call x1, Pallas kernels, shards(): pl.pallas_call(kernel, out_shape=jax.ShapeDtypeStruct((1024, 128), F32),...  121 us

profile of v1, /device:TPU:0, one launch (start us, length us, event | category | flops | bytes accessed | tf_op | source)
XLA Modules:
  0.0 123.7 jit_solution(7608475723114569872)
XLA Ops:
  0.7 121.2 %katz.1 = f32[1024,128]{1,0:T(8,128)} custom-call(bf16[128,128,128]{2,1,0:T(8,128)(2,1)} %bitcast.5, s32[1,128]{1,0:T(1,128)} %bitcast.6, s32[1,128]{1,0:T(1,128)} %bitcast.7, s32[1,1]{1,0:T(1,128)S(6)} %copy.8.count, s32[1,128]{1,0:T(1,128)} %bitcast.8, f32[1,128]{1,0:T(1,128)} %bitcast.9), custom_call_target="tpu_custom_call" | custom-call | tf_op jit(solution)/shard_map/katz/pallas_call | solution.py:291
  121.8 1.9 %copy.9 = f32[1024,128]{1,0:T(8,128)} copy(f32[1024,128]{1,0:T(8,128)} %katz.1) | data formatting | bytes 1048576

commit v2 on v1

v2 whole, which is shorter than its diff:
```python
import functools

import jax
import jax.numpy as jnp
from jax import lax
from jax.experimental import pallas as pl
from jax.experimental.pallas import tpu as pltpu
from jax.sharding import PartitionSpec as P

TERMS = 4
GROUP = 2
CHUNKS = 8
ROWS = 128 // CHUNKS
SLOTS = 128
NONE = 128
EMPTY = 48
UNROLL = 64
FIRST = 1
MERGE, FINISH, HAND_ON, NEXT = 0.28, 0.55, 0.85, 0.99
LATER, SPREAD = 0.06, 1.0
PERM, SCOL, KEEP, DEND, PKEND, SBASE, JIDX = range(7)
MESH = pl.DeviceIdType.MESH
BF16, F32, I32 = jnp.bfloat16, jnp.float32, jnp.int32


def down(row):
    return jnp.transpose(jnp.broadcast_to(row, (128, 128)))


def slot_tables(rows, cols, count, col_index):
    lane = lax.broadcasted_iota(I32, (128, 128), 1)
    sub = lax.broadcasted_iota(I32, (128, 128), 0)
    lane1 = lax.broadcasted_iota(I32, (1, 128), 1)
    key = jnp.where(lane1 < count, rows, 128)
    key_row = jnp.broadcast_to(key, (128, 128))
    key_col = down(key)

    def total(mask, value=1):
        return jnp.sum(jnp.where(mask, value, 0), axis=0, keepdims=True)

    earlier = (key_col == key_row) & (sub < lane)
    rank = total((key_col < key_row) | earlier)
    repeat = jnp.minimum(total(earlier), 1)
    place = down(rank) == lane
    perm = total(place, sub)
    scol = total(place, down(cols))
    keep = total(place, down(repeat))
    touched = total(key_col == lane) > 0
    upto = total(key_col <= lane)
    dend = jnp.where(touched, upto - 1, NONE)
    touched_col = down(touched.astype(I32)) > 0
    before = total(touched_col & ((sub >> 3) == (lane >> 3)) & (sub < lane))
    jidx = jnp.where(touched, before, 4)
    packed = touched_col & ((sub >> 3) == (lane >> 2)) & (down(before) == (lane & 3))
    ends = total(packed, down(upto))
    pkend = jnp.where(ends > 0, ends - 1, NONE)
    sbase = (((scol >> 3) * 16 + col_index) * 8 + (scol & 7)) * 128
    return jnp.concatenate([perm, scol, keep, dend, pkend, sbase, jidx, jidx], axis=0)


def kernel(tiles_hbm, trow, tcol, count, qids, damping, out, *scratch):
    scratch = list(scratch)
    take = lambda n: [scratch.pop(0) for _ in range(n)]
    raw, flip, tabv, tabs, metav, idxv, idxs, qmat, coef, own, score = take(11)
    run = take(CHUNKS // GROUP)
    xg = [take(CHUNKS) for _ in range(2)]
    recv1 = [take(CHUNKS) for _ in range(2)]
    send1, send2, recv2 = take(3)
    tile_sem, copy_sem, meta_ss, meta_rs, ss1, rs1, ss2, rs2, zss, zrs, css, crs = take(12)

    row, col = lax.axis_index("row"), lax.axis_index("col")
    z, core = row // 2, row % 2
    x, y = col // 4, col % 4
    wrap = lambda v, d: (v + d) % 4
    along = (
        lambda d: {"row": row, "col": wrap(x, d) * 4 + y},
        lambda d: {"row": row, "col": x * 4 + wrap(y, d)},
    )
    up = lambda d: {"row": wrap(z, d) * 2 + core, "col": col}
    other = {"row": z * 2 + 1 - core, "col": col}

    load = pltpu.make_async_copy(tiles_hbm, raw, tile_sem)
    load.start()
    barrier = pltpu.get_barrier_semaphore()
    peers = [f(d) for f in (*along, up) for d in (1, 2, 3)] + [other]
    for peer in peers:
        pl.semaphore_signal(barrier, inc=1, device_id=peer, device_id_type=MESH)

    def remote(src, dst, send_sem, recv_sem, peer):
        return pltpu.make_async_remote_copy(
            src_ref=src, dst_ref=dst, send_sem=send_sem, recv_sem=recv_sem, device_id=peer, device_id_type=MESH
        )

    tabv[...] = slot_tables(trow[...], tcol[...], count[0, 0], col)
    to_scalar = pltpu.make_async_copy(tabv, tabs, copy_sem.at[0])
    to_scalar.start()
    lane = lax.broadcasted_iota(I32, (128, 128), 1)
    qmat[...] = down(qids[...]) - lane
    coef[...] = down(damping[...])
    for g in range(CHUNKS // GROUP):
        run[g][NONE] = jnp.zeros((GROUP * ROWS, 128), BF16)
    for h in range(CHUNKS):
        for parity in range(2):
            recv1[parity][h][EMPTY] = jnp.zeros((ROWS, 128), BF16)
    to_scalar.wait()
    load.wait()

    def first_products():
        def body(step, total):
            for u in range(8):
                s = step * (8) + u
                tile = raw[tabs[PERM, s]]
                hot = (qmat[...] == tabs[SBASE, s]).astype(BF16)
                prod = lax.dot_general(hot, tile, (((1,), (1,)), ((), ())), preferred_element_type=F32)
                total = jnp.where(tabs[KEEP, s] > 0, prod + total, prod)
                rounded = total.astype(BF16)
                for g in range(CHUNKS // GROUP):
                    run[g][s] = rounded[g * GROUP * ROWS : (g + 1) * GROUP * ROWS]
                flip[s] = jnp.transpose(tile)
            return total

        lax.fori_loop(0, SLOTS // (8), body, jnp.zeros((128, 128), F32))

    def products(t, g):
        sources = [xg[(t - 1) % 2][g * GROUP + i] for i in range(GROUP)]

        def body(step, total):
            for u in range(UNROLL):
                s = step * UNROLL + u
                left = jnp.concatenate([source[tabs[SCOL, s]] for source in sources], axis=0)
                prod = jnp.dot(left, flip[s], preferred_element_type=F32)
                total = jnp.where(tabs[KEEP, s] > 0, prod + total, prod)
                run[g][s] = total.astype(BF16)
            return total

        lax.fori_loop(0, SLOTS // UNROLL, body, jnp.zeros((GROUP * ROWS, 128), F32))

    def part(h, index):
        return run[h // GROUP][index, pl.ds(h % GROUP * ROWS, ROWS), :]

    copies = {}

    odd = (x + y + core) % 2
    second = (
        (x + 2 * odd, y + 2 * (1 - odd)),
        (x + 1 - odd, y + odd),
        (x + 3 * (1 - odd), y + 3 * odd),
        (x, y),
    )
    second = [(u % 4) * 4 + v % 4 for u, v in second]

    def step1(t, h, axis, d):
        return remote(
            send1.at[h, axis, d - 1],
            recv1[t % 2][h].at[pl.ds(axis * 24 + (d - 1) * 8, 8)],
            ss1.at[t % 2, h, axis, d - 1],
            rs1.at[t % 2, h, axis, d - 1],
            along[axis](d),
        )

    def step2(t, h, k):
        return remote(
            send2.at[h, k], recv2.at[t % 2, h, k], ss2.at[t % 2, h, k], rs2.at[t % 2, h, k], {"row": row, "col": second[k]}
        )

    def ship(t, h):
        def body(d, _):
            flipped = (x + y + core + d) % 2
            for axis in range(2):
                for e in range(2):
                    if axis == 0:
                        dest = wrap(x, d) * 4 + wrap(y, flipped + 2 * e)
                    else:
                        dest = wrap(x, 1 - flipped + 2 * e) * 4 + wrap(y, d)
                    for j in range(4):
                        send1[h, axis, d - 1, e * 4 + j] = part(h, tabs[PKEND, dest * 4 + j])
                step1(t, h, axis, d).start()
            return 0

        lax.fori_loop(1, 4, body, 0)

    def merge(t, h):
        for d in (1, 2, 3):
            for axis in range(2):
                step1(t, h, axis, d).wait()

        def summed(k, b):
            block = second[k] * 8 + b
            axis = odd if k in (0, 3) else 1 - odd
            total = part(h, tabs[DEND, block]).astype(F32)
            for d in (1, 2, 3):
                total = total + recv1[t % 2][h][idxs[axis * 3 + d - 1, block]].astype(F32)
            return total

        for k in range(4):

            def body(b, _):
                if k < 3:
                    send2[h, k, b] = summed(k, b).astype(BF16)
                else:
                    own[h, b] = summed(k, b)
                return 0

            lax.fori_loop(0, 8, body, 0, unroll=4)
            if k < 3:
                step2(t, h, k).start()

    def finish(t, h):
        for k in range(3):
            step2(t, h, k).wait()
        base = pl.multiple_of(row * 8, 8)
        queries = pl.ds(h * ROWS, ROWS)
        factor = coef[queries, :]
        for _ in range(t - 1):
            factor = factor * coef[queries, :]

        def body(b, _):
            total = own[h, b]
            for k in range(3):
                total = total + recv2[t % 2, h, k, b].astype(F32)
            if t == 0:
                score[b, queries, :] = total
            else:
                score[b, queries, :] = score[b, queries, :] + factor * total
            if t + 1 < TERMS:
                xg[t % 2][h][base + b] = total.astype(BF16)
            return 0

        lax.fori_loop(0, 8, body, 0, unroll=4)
        if t + 1 < TERMS:
            mine = xg[t % 2][h].at[pl.ds(base, 8)]
            for d in (1, 2, 3):
                c = remote(mine, mine, zss.at[t % 2, h, d - 1], zrs.at[t % 2, h, d - 1], up(d))
                c.start()
                copies[3, t, h, d] = c
            c = remote(mine, mine, css.at[t % 2, h, 0], crs.at[t % 2, h, 0], other)
            c.start()
            copies[4, t, h, 0] = c

    def hand_on(t, h):
        for d in (1, 3, 2):
            copies[3, t, h, d].wait()
            source = pl.multiple_of((wrap(z, 4 - d) * 2 + core) * 8, 8)
            part = xg[t % 2][h].at[pl.ds(source, 8)]
            c = remote(part, part, css.at[t % 2, h, d], crs.at[t % 2, h, d], other)
            c.start()
            copies[4, t, h, d] = c

    def gathered(t, h):
        for d in range(4):
            copies[4, t, h, d].wait()

    first_products()
    pl.semaphore_wait(barrier, len(peers))
    meta = []
    for half in range(2):
        for d in (1, 2, 3):
            at = half * 3 + d - 1
            meta.append(remote(tabv, metav.at[at], meta_ss.at[at], meta_rs.at[at], along[half](d)))
            meta[-1].start()
    for h in range(FIRST):
        ship(0, h)
    for c in meta:
        c.wait()
    lane1 = lax.broadcasted_iota(I32, (1, 128), 1)
    for axis in range(2):
        for d in (1, 2, 3):
            at = axis * 3 + d - 1
            place = metav[at, JIDX : JIDX + 1, :]
            away = ((lane1 >> 3) & 3) - y - odd if axis == 0 else (lane1 >> 5) - x - 1 + odd
            which = ((away + 8) & 3) >> 1
            idxv[at : at + 1, :] = jnp.where(place < 4, axis * 24 + (d - 1) * 8 + which * 4 + place, EMPTY)
    idxv[6:8, :] = jnp.zeros((2, 128), I32)
    to_scalar = pltpu.make_async_copy(idxv, idxs, copy_sem.at[1])
    to_scalar.start()
    to_scalar.wait()
    def compute(t, g):
        chunks = range(g * GROUP, (g + 1) * GROUP)
        if t:
            for h in chunks:
                gathered(t - 1, h)
            products(t, g)
        for h in chunks:
            if t or h >= FIRST:
                ship(t, h)

    steps = []
    for t in range(TERMS):
        for g in range(CHUNKS // GROUP):
            start = t + g * GROUP / CHUNKS * (1 if t else SPREAD)
            steps.append((start + NEXT - 1, 3, compute, t, g))
            for i in range(GROUP):
                at, h = start + i * LATER, g * GROUP + i
                steps += [(at + MERGE, 0, merge, t, h), (at + FINISH, 1, finish, t, h)]
                if t + 1 < TERMS:
                    steps.append((at + HAND_ON, 2, hand_on, t, h))
    steps.sort(key=lambda step: (round(step[0], 6), step[1]))
    for _, _, step, t, h in steps:
        step(t, h)
    for b in range(8):
        out[b * 128 : (b + 1) * 128, :] = jnp.transpose(score[b])


def shards(tiles, tile_row, tile_col, tile_count, query_ids, damping):
    vmem = pl.BlockSpec(memory_space=pltpu.VMEM)
    dma = pltpu.SemaphoreType.DMA
    return pl.pallas_call(
        kernel,
        out_shape=jax.ShapeDtypeStruct((1024, 128), F32),
        in_specs=[pl.BlockSpec(memory_space=pl.ANY), vmem, vmem, pl.BlockSpec(memory_space=pltpu.SMEM), vmem, vmem],
        out_specs=vmem,
        scratch_shapes=[
            pltpu.VMEM((SLOTS, 128, 128), BF16),
            pltpu.VMEM((SLOTS, 128, 128), BF16),
            pltpu.VMEM((8, 128), I32),
            pltpu.SMEM((8, 128), I32),
            pltpu.VMEM((6, 8, 128), I32),
            pltpu.VMEM((8, 128), I32),
            pltpu.SMEM((8, 128), I32),
            pltpu.VMEM((128, 128), I32),
            pltpu.VMEM((128, 128), F32),
            pltpu.VMEM((CHUNKS, 8, ROWS, 128), F32),
            pltpu.VMEM((8, 128, 128), F32),
            *[pltpu.VMEM((SLOTS + 1, GROUP * ROWS, 128), BF16) for _ in range(CHUNKS // GROUP)],
            *[pltpu.VMEM((64, ROWS, 128), BF16) for _ in range(2 * CHUNKS)],
            *[pltpu.VMEM((EMPTY + 1, ROWS, 128), BF16) for _ in range(2 * CHUNKS)],
            pltpu.VMEM((CHUNKS, 2, 3, 8, ROWS, 128), BF16),
            pltpu.VMEM((CHUNKS, 3, 8, ROWS, 128), BF16),
            pltpu.VMEM((2, CHUNKS, 3, 8, ROWS, 128), BF16),
            dma,
            dma((2,)),
            dma((6,)),
            dma((6,)),
            dma((2, CHUNKS, 2, 3)),
            dma((2, CHUNKS, 2, 3)),
            dma((2, CHUNKS, 3)),
            dma((2, CHUNKS, 3)),
            dma((2, CHUNKS, 3)),
            dma((2, CHUNKS, 3)),
            dma((2, CHUNKS, 4)),
            dma((2, CHUNKS, 4)),
        ],
        compiler_params=pltpu.CompilerParams(collective_id=0, has_side_effects=True, vmem_limit_bytes=60 * 2**20),
        name="katz",
    )(
        tiles.reshape(SLOTS, 128, 128),
        tile_row.reshape(1, SLOTS),
        tile_col.reshape(1, SLOTS),
        tile_count,
        query_ids.reshape(1, 128),
        damping.reshape(1, 128),
    )


def solution(mesh):
    in_specs = (
        P("row", "col", None, None, None),
        P("row", "col", None),
        P("row", "col", None),
        P("row", "col"),
        P(),
        P(),
    )
    out_specs = P(("row", "col"), None)
    return jax.shard_map(shards, mesh=mesh, in_specs=in_specs, out_specs=out_specs, check_vma=False)
```

time: 124 us -> 106 us (0.85)
  Pallas kernels: 121 us -> 103 us
    pallas_call x1, Pallas kernels: 121 us -> 103 us  [shards(): pl.pallas_call(kernel, out_shape=jax.ShapeDtypeStruct((1024, 128), F32),...]
where the time goes in v2:
time: 106 us
  Pallas kernels  103 us (97%)
  local copies, waits for them, and re-layouts  1.87 us (2%)
    pallas_call x1, Pallas kernels, shards(): pl.pallas_call(kernel, out_shape=jax.ShapeDtypeStruct((1024, 128), F32),...  103 us

profile of v2, /device:TPU:0, one launch (start us, length us, event | category | flops | bytes accessed | tf_op | source)
XLA Modules:
  0.0 105.9 jit_solution(15646339251427445738)
XLA Ops:
  0.7 103.3 %katz.1 = f32[1024,128]{1,0:T(8,128)} custom-call(bf16[128,128,128]{2,1,0:T(8,128)(2,1)} %bitcast.5, s32[1,128]{1,0:T(1,128)} %bitcast.6, s32[1,128]{1,0:T(1,128)} %bitcast.7, s32[1,1]{1,0:T(1,128)S(6)} %copy.8.count, s32[1,128]{1,0:T(1,128)} %bitcast.8, f32[1,128]{1,0:T(1,128)} %bitcast.9), custom_call_target="tpu_custom_call" | custom-call | tf_op jit(solution)/shard_map/katz/pallas_call | solution.py:307
  104.0 1.9 %copy.9 = f32[1024,128]{1,0:T(8,128)} copy(f32[1024,128]{1,0:T(8,128)} %katz.1) | data formatting | bytes 1048576

commit v3 on v2

--- a/solution.py
+++ b/solution.py
@@ -8,16 +8,18 @@
 from jax.sharding import PartitionSpec as P
 
 TERMS = 4
-GROUP = 2
+PACK = 32
+GROUP = 1
 CHUNKS = 8
 ROWS = 128 // CHUNKS
 SLOTS = 128
 NONE = 128
 EMPTY = 48
-UNROLL = 64
+EMPTY0 = 60
+FIRST_UNROLL = 8
 FIRST = 1
-MERGE, FINISH, HAND_ON, NEXT = 0.28, 0.55, 0.85, 0.99
-LATER, SPREAD = 0.06, 1.0
+MERGE, FINISH, HAND_ON, NEXT = 0.26, 0.53, 0.8, 0.99
+LATER, SPREAD = 0.0, 1.0
 PERM, SCOL, KEEP, DEND, PKEND, SBASE, JIDX = range(7)
 MESH = pl.DeviceIdType.MESH
 BF16, F32, I32 = jnp.bfloat16, jnp.float32, jnp.int32
@@ -58,7 +60,7 @@
     return jnp.concatenate([perm, scol, keep, dend, pkend, sbase, jidx, jidx], axis=0)
 
 
-def kernel(tiles_hbm, trow, tcol, count, qids, damping, out, *scratch):
+def kernel(short, tiles_hbm, trow, tcol, count, qids, damping, out, *scratch):
     scratch = list(scratch)
     take = lambda n: [scratch.pop(0) for _ in range(n)]
     raw, flip, tabv, tabs, metav, idxv, idxs, qmat, coef, own, score = take(11)
@@ -67,6 +69,8 @@
     recv1 = [take(CHUNKS) for _ in range(2)]
     send1, send2, recv2 = take(3)
     tile_sem, copy_sem, meta_ss, meta_rs, ss1, rs1, ss2, rs2, zss, zrs, css, crs = take(12)
+    if short:
+        run0, send0, recv0, idx0v, idx0s, place0, ss0, rs0 = take(8)
 
     row, col = lax.axis_index("row"), lax.axis_index("col")
     z, core = row // 2, row % 2
@@ -76,13 +80,16 @@
         lambda d: {"row": row, "col": wrap(x, d) * 4 + y},
         lambda d: {"row": row, "col": x * 4 + wrap(y, d)},
     )
+    across = lambda k: {"row": row, "col": wrap(x, k // 4) * 4 + wrap(y, k % 4)}
+    near = [4, 8, 12, 1, 2, 3]
+    greeted = range(1, 16) if short else near
     up = lambda d: {"row": wrap(z, d) * 2 + core, "col": col}
     other = {"row": z * 2 + 1 - core, "col": col}
 
     load = pltpu.make_async_copy(tiles_hbm, raw, tile_sem)
     load.start()
     barrier = pltpu.get_barrier_semaphore()
-    peers = [f(d) for f in (*along, up) for d in (1, 2, 3)] + [other]
+    peers = [across(k) for k in greeted] + [up(d) for d in (1, 2, 3)] + [other]
     for peer in peers:
         pl.semaphore_signal(barrier, inc=1, device_id=peer, device_id_type=MESH)
 
@@ -95,7 +102,23 @@
     to_scalar = pltpu.make_async_copy(tabv, tabs, copy_sem.at[0])
     to_scalar.start()
     lane = lax.broadcasted_iota(I32, (128, 128), 1)
-    qmat[...] = down(qids[...]) - lane
+    if short:
+        sub = lax.broadcasted_iota(I32, (128, 128), 0)
+        queries = qids[...]
+        owner = (queries >> 10) & 15
+        owner_col = down(owner)
+        rank = jnp.sum(jnp.where((owner_col == owner) & (sub < lane), 1, 0), axis=0, keepdims=True)
+        packed = (owner_col == col) & (down(rank) == lane)
+        ids = jnp.sum(jnp.where(packed, down(queries) + 1, 0), axis=0, keepdims=True)
+        qmat[...] = down(jnp.where(ids > 0, ids - 1, -(2**20))) - lane
+        source = ((x - (owner >> 2) + 4) & 3) * 4 + ((y - (owner & 3) + 4) & 3)
+        target = down(source * PACK + rank)
+        for m in range(4):
+            place0[:, m * 128 : (m + 1) * 128] = (target == lane + m * 128).astype(F32).astype(BF16)
+        run0[NONE] = jnp.zeros((PACK, 128), BF16)
+        recv0[EMPTY0] = jnp.zeros((PACK, 128), BF16)
+    else:
+        qmat[...] = down(qids[...]) - lane
     coef[...] = down(damping[...])
     for g in range(CHUNKS // GROUP):
         run[g][NONE] = jnp.zeros((GROUP * ROWS, 128), BF16)
@@ -106,34 +129,41 @@
     load.wait()
 
     def first_products():
+        height = PACK if short else 128
+
         def body(step, total):
-            for u in range(8):
-                s = step * (8) + u
+            for u in range(FIRST_UNROLL):
+                s = step * FIRST_UNROLL + u
                 tile = raw[tabs[PERM, s]]
-                hot = (qmat[...] == tabs[SBASE, s]).astype(BF16)
+                hot = (qmat[0:height, :] == tabs[SBASE, s]).astype(BF16)
                 prod = lax.dot_general(hot, tile, (((1,), (1,)), ((), ())), preferred_element_type=F32)
                 total = jnp.where(tabs[KEEP, s] > 0, prod + total, prod)
                 rounded = total.astype(BF16)
-                for g in range(CHUNKS // GROUP):
-                    run[g][s] = rounded[g * GROUP * ROWS : (g + 1) * GROUP * ROWS]
+                if short:
+                    run0[s] = rounded
+                else:
+                    for g in range(CHUNKS // GROUP):
+                        run[g][s] = rounded[g * GROUP * ROWS : (g + 1) * GROUP * ROWS]
                 flip[s] = jnp.transpose(tile)
             return total
 
-        lax.fori_loop(0, SLOTS // (8), body, jnp.zeros((128, 128), F32))
+        lax.fori_loop(0, SLOTS // FIRST_UNROLL, body, jnp.zeros((height, 128), F32))
+
+    unroll = 64 if short else 2
 
     def products(t, g):
         sources = [xg[(t - 1) % 2][g * GROUP + i] for i in range(GROUP)]
 
         def body(step, total):
-            for u in range(UNROLL):
-                s = step * UNROLL + u
+            for u in range(unroll):
+                s = step * unroll + u
                 left = jnp.concatenate([source[tabs[SCOL, s]] for source in sources], axis=0)
                 prod = jnp.dot(left, flip[s], preferred_element_type=F32)
                 total = jnp.where(tabs[KEEP, s] > 0, prod + total, prod)
                 run[g][s] = total.astype(BF16)
             return total
 
-        lax.fori_loop(0, SLOTS // UNROLL, body, jnp.zeros((GROUP * ROWS, 128), F32))
+        lax.fori_loop(0, SLOTS // unroll, body, jnp.zeros((GROUP * ROWS, 128), F32))
 
     def part(h, index):
         return run[h // GROUP][index, pl.ds(h % GROUP * ROWS, ROWS), :]
@@ -201,7 +231,7 @@
                     own[h, b] = summed(k, b)
                 return 0
 
-            lax.fori_loop(0, 8, body, 0, unroll=4)
+            lax.fori_loop(0, 8, body, 0, unroll=4 if short else 1)
             if k < 3:
                 step2(t, h, k).start()
 
@@ -226,16 +256,51 @@
                 xg[t % 2][h][base + b] = total.astype(BF16)
             return 0
 
-        lax.fori_loop(0, 8, body, 0, unroll=4)
+        lax.fori_loop(0, 8, body, 0, unroll=4 if short else 1)
         if t + 1 < TERMS:
-            mine = xg[t % 2][h].at[pl.ds(base, 8)]
-            for d in (1, 2, 3):
-                c = remote(mine, mine, zss.at[t % 2, h, d - 1], zrs.at[t % 2, h, d - 1], up(d))
-                c.start()
-                copies[3, t, h, d] = c
-            c = remote(mine, mine, css.at[t % 2, h, 0], crs.at[t % 2, h, 0], other)
+            spread(t, h)
+
+    def spread(t, h):
+        mine = xg[t % 2][h].at[pl.ds(pl.multiple_of(row * 8, 8), 8)]
+        for d in (1, 2, 3):
+            c = remote(mine, mine, zss.at[t % 2, h, d - 1], zrs.at[t % 2, h, d - 1], up(d))
             c.start()
-            copies[4, t, h, 0] = c
+            copies[3, t, h, d] = c
+        c = remote(mine, mine, css.at[t % 2, h, 0], crs.at[t % 2, h, 0], other)
+        c.start()
+        copies[4, t, h, 0] = c
+
+    def step0(k):
+        return remote(
+            send0.at[k - 1], recv0.at[pl.ds((k - 1) * 4, 4)], ss0.at[k - 1], rs0.at[k - 1], across(k)
+        )
+
+    def ship_short():
+        def body(k, _):
+            dest = wrap(x, k // 4) * 4 + wrap(y, k % 4)
+            for j in range(4):
+                send0[k - 1, j] = run0[tabs[PKEND, dest * 4 + j]]
+            step0(k).start()
+            return 0
+
+        lax.fori_loop(1, 16, body, 0)
+
+    def finish_short():
+        for k in range(1, 16):
+            step0(k).wait()
+        base = pl.multiple_of(row * 8, 8)
+
+        def body(b, _):
+            block = col * 8 + b
+            parts = [run0[tabs[DEND, block]]] + [recv0[idx0s[k - 1, block]] for k in range(1, 16)]
+            total = jnp.dot(place0[...], jnp.concatenate(parts, axis=0), preferred_element_type=F32)
+            score[b] = total
+            rounded = total.astype(BF16)
+            for h in range(CHUNKS):
+                xg[0][h][base + b] = rounded[h * ROWS : (h + 1) * ROWS]
+            return 0
+
+        lax.fori_loop(0, 8, body, 0)
 
     def hand_on(t, h):
         for d in (1, 3, 2):
@@ -253,27 +318,40 @@
     first_products()
     pl.semaphore_wait(barrier, len(peers))
     meta = []
-    for half in range(2):
-        for d in (1, 2, 3):
-            at = half * 3 + d - 1
-            meta.append(remote(tabv, metav.at[at], meta_ss.at[at], meta_rs.at[at], along[half](d)))
-            meta[-1].start()
-    for h in range(FIRST):
-        ship(0, h)
+    for at, k in enumerate(greeted):
+        meta.append(remote(tabv, metav.at[at], meta_ss.at[at], meta_rs.at[at], across(k)))
+        meta[-1].start()
+    if short:
+        ship_short()
+    else:
+        for h in range(FIRST):
+            ship(0, h)
     for c in meta:
         c.wait()
     lane1 = lax.broadcasted_iota(I32, (1, 128), 1)
     for axis in range(2):
         for d in (1, 2, 3):
             at = axis * 3 + d - 1
-            place = metav[at, JIDX : JIDX + 1, :]
+            place = metav[near[at] - 1 if short else at, JIDX : JIDX + 1, :]
             away = ((lane1 >> 3) & 3) - y - odd if axis == 0 else (lane1 >> 5) - x - 1 + odd
             which = ((away + 8) & 3) >> 1
             idxv[at : at + 1, :] = jnp.where(place < 4, axis * 24 + (d - 1) * 8 + which * 4 + place, EMPTY)
     idxv[6:8, :] = jnp.zeros((2, 128), I32)
     to_scalar = pltpu.make_async_copy(idxv, idxs, copy_sem.at[1])
     to_scalar.start()
+    if short:
+        for k in range(1, 16):
+            place = metav[k - 1, JIDX : JIDX + 1, :]
+            idx0v[k - 1 : k, :] = jnp.where(place < 4, (k - 1) * 4 + place, EMPTY0)
+        idx0v[15:16, :] = jnp.zeros((1, 128), I32)
+        to_scalar0 = pltpu.make_async_copy(idx0v, idx0s, copy_sem.at[2])
+        to_scalar0.start()
+        to_scalar0.wait()
     to_scalar.wait()
+    if short:
+        finish_short()
+        for h in range(CHUNKS):
+            spread(0, h)
     def compute(t, g):
         chunks = range(g * GROUP, (g + 1) * GROUP)
         if t:
@@ -288,10 +366,12 @@
     for t in range(TERMS):
         for g in range(CHUNKS // GROUP):
             start = t + g * GROUP / CHUNKS * (1 if t else SPREAD)
-            steps.append((start + NEXT - 1, 3, compute, t, g))
+            if t or not short:
+                steps.append((start + NEXT - 1, 3, compute, t, g))
             for i in range(GROUP):
                 at, h = start + i * LATER, g * GROUP + i
-                steps += [(at + MERGE, 0, merge, t, h), (at + FINISH, 1, finish, t, h)]
+                if t or not short:
+                    steps += [(at + MERGE, 0, merge, t, h), (at + FINISH, 1, finish, t, h)]
                 if t + 1 < TERMS:
                     steps.append((at + HAND_ON, 2, hand_on, t, h))
     steps.sort(key=lambda step: (round(step[0], 6), step[1]))
@@ -301,11 +381,24 @@
         out[b * 128 : (b + 1) * 128, :] = jnp.transpose(score[b])
 
 
-def shards(tiles, tile_row, tile_col, tile_count, query_ids, damping):
+def short_scratch():
+    return (
+        pltpu.VMEM((SLOTS + 1, PACK, 128), BF16),
+        pltpu.VMEM((15, 4, PACK, 128), BF16),
+        pltpu.VMEM((EMPTY0 + 1, PACK, 128), BF16),
+        pltpu.VMEM((16, 128), I32),
+        pltpu.SMEM((16, 128), I32),
+        pltpu.VMEM((128, 512), BF16),
+        pltpu.SemaphoreType.DMA((15,)),
+        pltpu.SemaphoreType.DMA((15,)),
+    )
+
+
+def call(short, tiles, tile_row, tile_col, tile_count, query_ids, damping):
     vmem = pl.BlockSpec(memory_space=pltpu.VMEM)
     dma = pltpu.SemaphoreType.DMA
     return pl.pallas_call(
-        kernel,
+        functools.partial(kernel, short),
         out_shape=jax.ShapeDtypeStruct((1024, 128), F32),
         in_specs=[pl.BlockSpec(memory_space=pl.ANY), vmem, vmem, pl.BlockSpec(memory_space=pltpu.SMEM), vmem, vmem],
         out_specs=vmem,
@@ -314,7 +407,7 @@
             pltpu.VMEM((SLOTS, 128, 128), BF16),
             pltpu.VMEM((8, 128), I32),
             pltpu.SMEM((8, 128), I32),
-            pltpu.VMEM((6, 8, 128), I32),
+            pltpu.VMEM((15 if short else 6, 8, 128), I32),
             pltpu.VMEM((8, 128), I32),
             pltpu.SMEM((8, 128), I32),
             pltpu.VMEM((128, 128), I32),
@@ -328,9 +421,9 @@
             pltpu.VMEM((CHUNKS, 3, 8, ROWS, 128), BF16),
             pltpu.VMEM((2, CHUNKS, 3, 8, ROWS, 128), BF16),
             dma,
-            dma((2,)),
-            dma((6,)),
-            dma((6,)),
+            dma((3,)),
+            dma((15,)),
+            dma((15,)),
             dma((2, CHUNKS, 2, 3)),
             dma((2, CHUNKS, 2, 3)),
             dma((2, CHUNKS, 3)),
@@ -339,9 +432,10 @@
             dma((2, CHUNKS, 3)),
             dma((2, CHUNKS, 4)),
             dma((2, CHUNKS, 4)),
+            *(short_scratch() if short else ()),
         ],
-        compiler_params=pltpu.CompilerParams(collective_id=0, has_side_effects=True, vmem_limit_bytes=60 * 2**20),
-        name="katz",
+        compiler_params=pltpu.CompilerParams(collective_id=int(short), has_side_effects=True, vmem_limit_bytes=60 * 2**20),
+        name="katz_short" if short else "katz",
     )(
         tiles.reshape(SLOTS, 128, 128),
         tile_row.reshape(1, SLOTS),
@@ -350,6 +444,13 @@
         query_ids.reshape(1, 128),
         damping.reshape(1, 128),
     )
+
+
+def shards(tiles, tile_row, tile_col, tile_count, query_ids, damping):
+    owner = (query_ids >> 10) & 15
+    held = jnp.sum((owner[:, None] == jnp.arange(16, dtype=I32)[None, :]).astype(I32), axis=0)
+    args = (tiles, tile_row, tile_col, tile_count, query_ids, damping)
+    return lax.cond(jnp.max(held) <= PACK, functools.partial(call, True), functools.partial(call, False), *args)
 
 
 def solution(mesh):

time: 106 us -> 99.2 us (0.936)
  Pallas kernels: 103 us -> 95.8 us
  other arithmetic: 0 us -> 1.41 us
  local copies, waits for them, and re-layouts: 1.87 us -> 0.8 us
    pallas_call x1, Pallas kernels: 103 us -> 95.8 us  [call(): pl.pallas_call(functools.partial(kernel, short), out_shape=jax.ShapeDtype...]
    unnamed x1, local copies, waits for them, and re-layouts: 1.87 us -> 0.8 us
where the time goes in v3:
time: 99.2 us; the launch traced here: 99 us
  Pallas kernels  95.8 us (97%)
  other arithmetic  1.41 us (1%)
    pallas_call x1, Pallas kernels, call(): pl.pallas_call(functools.partial(kernel, short), out_shape=jax.ShapeDtype...  95.8 us

profile of v3, /device:TPU:0, one launch (start us, length us, event | category | flops | bytes accessed | tf_op | source)
XLA Modules:
  0.0 99.0 jit_solution(3573227734484920785)
XLA Ops:
  0.0 0.7 shift-right-arithmetic_and_fusion
  0.7 0.1 convert_reduce_fusion
  0.8 0.6 reduce_max.9
  2.1 96.1 %conditional.1 = (f32[1024,128]{1,0:T(8,128)S(1)}) conditional(s32[]{:T(128)} %convert_element_type.7, (bf16[1,1,128,128,128]{4,3,2,1,0:T(8,128)(2,1)}, s32[1,1,128]{2,1,0:T(1,128)}, s32[1,1,128]{2,1,0:T(1,128)}, s32[128]{0:T(128)}, f32[128]{0:T(128)}, /*index=5*/s32[1,1]{1,0:T(1,128)}) %tuple.11, (bf16[1,1,128,128,128]{4,3,2,1,0:T(8,128)(2,1)}, ...), branch_computations={%region_2.0_spmd, %region_3.0_spmd} | conditional | bytes 8 | solution.py:453
  2.1 95.8 %katz_short.1 = f32[1024,128]{1,0:T(8,128)S(1)} custom-call(bf16[128,128,128]{2,1,0:T(8,128)(2,1)} %bitcast.11, s32[1,128]{1,0:T(1,128)} %bitcast.15, s32[1,128]{1,0:T(1,128)} %bitcast.17, s32[1,1]{1,0:T(1,128)} %get-tuple-element.41.count, s32[1,128]{1,0:T(1,128)} %bitcast.13, f32[1,128]{1,0:T(1,128)} %bitcast.19), custom_call_target="tpu_custom_call" | custom-call | tf_op jit(solution)/shard_map/cond/branch_1_fun/katz_short/pallas_call | solution.py:400
  98.2 0.8 copy.12
